TPU v7x, 32 devices: a whole 2x2x4 slice. The times are simulated.
32 devices in a mesh: gx: 4 (over y, x), gy: 2 (over core), gz: 4 (over z).
Axes of the slice: x: 2, y: 2, z: 4, core: 2. Of those that a mesh axis runs over, the one named last changes fastest.
Arguments:
- volume: bfloat16 [32, 64, 64, 32], P('gx', 'gy', 'gz'), may hold values from -6 to 6
- conv_in: bfloat16 [3, 3, 3, 32, 32], replicated, may hold values from -0.21875 to 0.21875
- conv_out: bfloat16 [3, 3, 3, 32, 32], replicated, may hold values from -0.21875 to 0.21875
- norm_gain: float32 [256], replicated, may hold values from 0.1 to 1.9
- q_weight: bfloat16 [256, 256], replicated, may hold values from -3 to 3
- kv_weight: bfloat16 [256, 512], replicated, may hold values from -0.375 to 0.375
- out_weight: bfloat16 [256, 256], replicated, may hold values from -0.375 to 0.375
- up_weight: bfloat16 [256, 256], replicated, may hold values from -0.375 to 0.375
Outputs:
- joined_out: bfloat16 [32, 64, 64, 32], P('gx', 'gy', 'gz')
All inputs are finite; a program needn't handle non-finite values.
Results may differ from a plain program's by a relative error of at most 0.012.
The roundings to bfloat16 on the way count: a program that leaves them out, or rounds other values in their place, can miss the bound.
Values may be sent and summed in bfloat16 or wider, within the bound.
No kernel may reach another device: no remote copies, remote signals or barrier semaphores. Data moves between devices by JAX's collectives and lax.ppermute only.
A program may use at most 64 MiB of HBM per device.

v0:
```python
import math
import jax
import jax.numpy as jnp
from jax import lax
from jax.sharding import PartitionSpec as P

HEADS = 8


def with_halo(cells, sides, width):
    for axis, dim in sides:
        count = lax.axis_size(axis)
        ends = count - 1
        head = lax.slice_in_dim(cells, 0, width, axis=dim)
        tail = lax.slice_in_dim(cells, cells.shape[dim] - width, cells.shape[dim], axis=dim)
        cells = jnp.concatenate(
            [
                lax.ppermute(tail, axis, [(i, (i + 1) % count) for i in range(ends)]),
                cells,
                lax.ppermute(head, axis, [((i + 1) % count, i) for i in range(ends)]),
            ],
            axis=dim,
        )
    return cells


def convolve(padded, kernel):
    return lax.conv_general_dilated(
        padded[None],
        kernel,
        (1, 1, 1),
        "VALID",
        dimension_numbers=("NDHWC", "DHWIO", "NDHWC"),
        preferred_element_type=jnp.float32,
    )[0]


def pad_brick(brick):
    return with_halo(brick, (("gx", 0), ("gy", 1), ("gz", 2)), 1)


def tokenize(volume_map):
    extent_x, extent_y, extent_z, channels = volume_map.shape
    grid_cells = volume_map.reshape(
        extent_x // 8, 2, 4, extent_y // 8, 2, 4, extent_z // 8, 2, 4, channels
    ).mean(axis=(2, 5, 8))
    grid_cells = grid_cells.transpose(0, 2, 4, 1, 3, 5, 6)
    return grid_cells.reshape(extent_x // 8 * (extent_y // 8) * (extent_z // 8), 8 * channels)


def spread_cells(token_rows, extent_x, extent_y, extent_z):
    channels = token_rows.shape[1] // 8
    grid_cells = token_rows.reshape(
        extent_x // 8, extent_y // 8, extent_z // 8, 2, 2, 2, channels
    ).transpose(0, 3, 1, 4, 2, 5, 6)
    grid_cells = jnp.broadcast_to(
        grid_cells[:, :, None, :, :, None, :, :, None, :],
        (extent_x // 8, 2, 4, extent_y // 8, 2, 4, extent_z // 8, 2, 4, channels),
    )
    return grid_cells.reshape(extent_x, extent_y, extent_z, channels)


def layer_norm(tokens, norm_gain):
    center = tokens - tokens.mean(axis=1, keepdims=True)
    spread = (center * center).mean(axis=1, keepdims=True)
    return (center * lax.rsqrt(spread + 1e-05) * norm_gain).astype(jnp.bfloat16)


def make_folder(queries, running, shard_piece):
    scaling = queries.shape[-1] ** (-0.5)
    key_count = shard_piece.shape[2]
    block_rows = math.gcd(key_count, 1024)

    def advance(position, state):
        peak_score, denominator, numerator = state
        head_keys = lax.dynamic_slice_in_dim(shard_piece[0], position * block_rows, block_rows, 1)
        head_values = lax.dynamic_slice_in_dim(shard_piece[1], position * block_rows, block_rows, 1)
        scores = (
            jnp.einsum("hqd,hkd->hqk", queries, head_keys, preferred_element_type=jnp.float32)
            * scaling
        )
        new_peak = jnp.maximum(peak_score, scores.max(axis=-1))
        rescale = jnp.exp(peak_score - new_peak)
        weights = jnp.exp(scores - new_peak[..., None])
        denominator = denominator * rescale + weights.sum(axis=-1)
        numerator = numerator * rescale[..., None] + jnp.einsum(
            "hqk,hkd->hqd",
            weights.astype(jnp.bfloat16),
            head_values,
            preferred_element_type=jnp.float32,
        )
        return (new_peak, denominator, numerator)

    return lax.fori_loop(0, key_count // block_rows, advance, running)


def start_state(queries):
    heads_here, query_count, head_size = queries.shape
    return (
        jnp.full((heads_here, query_count), -1e30, jnp.float32),
        jnp.zeros((heads_here, query_count), jnp.float32),
        jnp.zeros((heads_here, query_count, head_size), jnp.float32),
    )


def finish(running):
    return (running[2] / running[1][..., None]).astype(jnp.bfloat16)


def on_device(volume, conv_in, conv_out, norm_gain, q_weight, kv_weight, out_weight, up_weight):
    extent_x, extent_y, extent_z, channels = volume.shape
    encoded = jax.nn.relu(convolve(pad_brick(volume), conv_in)).astype(jnp.bfloat16)
    tokens = tokenize(encoded.astype(jnp.float32))
    normed = layer_norm(tokens, norm_gain)
    queries = jnp.dot(normed, q_weight, preferred_element_type=jnp.float32).astype(jnp.bfloat16)
    key_value = jnp.dot(normed, kv_weight, preferred_element_type=jnp.float32).astype(jnp.bfloat16)
    token_count, width = tokens.shape
    head_size = width // HEADS
    packed = (
        jnp.concatenate([queries, key_value], axis=1)
        .reshape(token_count, 3, HEADS, head_size)
        .transpose(1, 2, 0, 3)
    )
    arranged = lax.all_to_all(packed, "gz", split_axis=1, concat_axis=2, tiled=True)
    head_queries = arranged[0]
    running = make_folder(
        head_queries,
        start_state(head_queries),
        lax.all_gather(arranged[1:], ("gx", "gy"), axis=2, tiled=True),
    )
    returned = lax.all_to_all(finish(running), "gz", split_axis=1, concat_axis=0, tiled=True)
    attended = returned.transpose(1, 0, 2).reshape(token_count, width)
    mixture = (tokens + jnp.dot(attended, out_weight, preferred_element_type=jnp.float32)).astype(
        jnp.bfloat16
    )
    upward = jnp.dot(mixture, up_weight, preferred_element_type=jnp.float32)
    joined = (
        encoded.astype(jnp.float32) + spread_cells(upward, extent_x, extent_y, extent_z)
    ).astype(jnp.bfloat16)
    return convolve(pad_brick(joined), conv_out).astype(jnp.bfloat16)


def solution(mesh):
    placed = (P("gx", "gy", "gz", None), P(), P(), P(), P(), P(), P(), P())
    return jax.shard_map(
        on_device, mesh=mesh, in_specs=placed, out_specs=P("gx", "gy", "gz", None), check_vma=False
    )
```

profile of v0, /device:TPU:0, one launch (start us, length us, event | category | flops | bytes accessed | tf_op | source)
XLA Modules:
  0.0 124.4 jit_solution(1911006101393436707)
XLA Ops:
  0.0 2.0 %copy.101 = bf16[8,32,16,32]{1,3,2,0:T(8,128)(2,1)S(1)} copy(bf16[8,32,16,32]{3,2,1,0:T(8,128)(2,1)} %param.8) | data formatting | bytes 524288 | tf_op args[0]
  2.0 4.9 %collective-permute-start = (bf16[1,32,16,32]{1,3,2,0:T(8,128)(2,1)S(1)}, bf16[1,32,16,32]{1,3,2,0:T(8,128)(2,1)S(1)}, u32[]{:S(2)}, u32[]{:S(2)}) collective-permute-start(bf16[1,32,16,32]{1,3,2,0:T(8,128)(2,1)S(1)} %get-tuple-element.36), channel_id=1, source_target_pairs={{0,8},{8,16},{16,24},{1,9},{9,17},{17,25},{2,10},{10,18},{18,26},{... | collective-permute-start | bytes 98312 | tf_op jit(solution)/shard_map/ppermute | solution.py:18
  8.2 1.4 %collective-permute-done = bf16[1,32,16,32]{1,3,2,0:T(8,128)(2,1)S(1)} collective-permute-done((bf16[1,32,16,32]{1,3,2,0:T(8,128)(2,1)S(1)}, bf16[1,32,16,32]{1,3,2,0:T(8,128)(2,1)S(1)}, u32[]{:S(2)}, u32[]{:S(2)}) %collective-permute-start) | collective-permute-done | bytes 32800 | tf_op jit(solution)/shard_map/ppermute | solution.py:18
  9.6 4.8 %collective-permute-done.1 = bf16[1,32,16,32]{1,3,2,0:T(8,128)(2,1)S(1)} collective-permute-done((bf16[1,32,16,32]{1,3,2,0:T(8,128)(2,1)S(1)}, bf16[1,32,16,32]{1,3,2,0:T(8,128)(2,1)S(1)}, u32[]{:S(2)}, u32[]{:S(2)}) %collective-permute-start.1) | collective-permute-done | bytes 32800 | tf_op jit(solution)/shard_map/ppermute | solution.py:20
  14.7 1.7 %fusion.43 = (bf16[10,1,16,32]{1,3,2,0:T(8,128)(2,1)}, bf16[10,1,16,32]{1,3,2,0:T(8,128)(2,1)S(1)}) fusion(bf16[10,32,16,32]{1,3,2,0:T(8,128)(2,1)S(1)} %pad_maximum_fusion), kind=kLoop, calls=%fused_computation.75 | loop fusion | bytes 40960 | tf_op jit(solution)/shard_map/slice | solution.py:15
  16.4 2.3 %copy.104 = bf16[10,1,16,32]{3,2,1,0:T(8,128)(2,1)S(1)} copy(bf16[10,1,16,32]{1,3,2,0:T(8,128)(2,1)} %get-tuple-element.32) | data formatting | bytes 20480 | tf_op jit(solution)/shard_map/slice | solution.py:15
  18.7 1.3 %collective-permute-start.2 = (bf16[10,1,16,32]{3,2,1,0:T(8,128)(2,1)S(1)}, bf16[10,1,16,32]{3,2,1,0:T(8,128)(2,1)S(1)}, u32[]{:S(2)}, u32[]{:S(2)}) collective-permute-start(bf16[10,1,16,32]{3,2,1,0:T(8,128)(2,1)S(1)} %copy.104), channel_id=1, source_target_pairs={{0,4},{1,5},{2,6},{3,7},{8,12},{9,13},{10,14},{11,15},{16,20},{17,... | collective-permute-start | bytes 30728 | tf_op jit(solution)/shard_map/ppermute | solution.py:18
  24.1 2.1 %copy.107 = bf16[10,1,16,32]{1,3,2,0:T(8,128)(2,1)} copy(bf16[10,1,16,32]{3,2,1,0:T(8,128)(2,1)S(1)} %collective-permute-done.3) | data formatting | bytes 20480 | tf_op jit(solution)/shard_map/ppermute | solution.py:20
  27.4 3.5 %collective-permute-start.4 = (bf16[10,34,1,32]{1,3,2,0:T(8,128)(2,1)S(1)}, bf16[10,34,1,32]{1,3,2,0:T(8,128)(2,1)S(1)}, u32[]{:S(2)}, u32[]{:S(2)}) collective-permute-start(bf16[10,34,1,32]{1,3,2,0:T(8,128)(2,1)S(1)} %get-tuple-element.17), channel_id=1, source_target_pairs={{0,1},{1,2},{2,3},{4,5},{5,6},{6,7},{8,9},{9,10},{10,11},{12,13},{... | collective-permute-start | bytes 65288 | tf_op jit(solution)/shard_map/ppermute | solution.py:18
  30.9 1.5 %collective-permute-start.5 = (bf16[10,34,1,32]{1,3,2,0:T(8,128)(2,1)S(1)}, bf16[10,34,1,32]{1,3,2,0:T(8,128)(2,1)S(1)}, u32[]{:S(2)}, u32[]{:S(2)}) collective-permute-start(bf16[10,34,1,32]{1,3,2,0:T(8,128)(2,1)S(1)} %get-tuple-element.18), channel_id=1, source_target_pairs={{1,0},{2,1},{3,2},{5,4},{6,5},{7,6},{9,8},{10,9},{11,10},{13,12},{... | collective-permute-start | bytes 65288 | tf_op jit(solution)/shard_map/ppermute | solution.py:20
  33.1 4.1 %collective-permute-done.5 = bf16[10,34,1,32]{1,3,2,0:T(8,128)(2,1)S(1)} collective-permute-done((bf16[10,34,1,32]{1,3,2,0:T(8,128)(2,1)S(1)}, bf16[10,34,1,32]{1,3,2,0:T(8,128)(2,1)S(1)}, u32[]{:S(2)}, u32[]{:S(2)}) %collective-permute-start.5) | collective-permute-done | bytes 21792 | tf_op jit(solution)/shard_map/ppermute | solution.py:20
  38.9 3.1 %copy.109 = bf16[10,34,1,8,3,32]{5,3,4,1,0,2:T(8,128)(2,1)} copy(bf16[10,34,1,8,3,32]{1,5,4,3,2,0:T(8,128)(2,1)S(1)} %bitcast.88) | data formatting | bytes 1044480 | tf_op jit(solution)/shard_map/conv_general_dilated | solution.py:28
  42.0 1.9 %slice.79 = bf16[10,34,1,7,2,32]{5,3,4,1,0,2:T(8,128)(2,1)S(1)} slice(bf16[10,34,1,8,3,32]{5,3,4,1,0,2:T(8,128)(2,1)} %copy.109), slice={[0:10], [0:34], [0:1], [1:8], [0:2], [0:32]} | slice | bytes 609280 | tf_op jit(solution)/shard_map/conv_general_dilated | solution.py:28
  44.0 4.4 %maximum_convert_fusion = bf16[8,32,8,3,32]{4,2,3,1,0:T(8,128)(2,1)S(1)} fusion(pred[8,3]{0,1:T(4,128)(4,1)S(1)} %copy-done.10, bf16[3,3,3,32,32]{4,3,2,1,0:T(8,128)(2,1)S(1)} %copy-done.6, bf16[10,34,1,7,2,32]{5,3,4,1,0,2:T(8,128)(2,1)S(1)} %slice.79, bf16[10,34,1,8,3,32]{5,3,4,1,0,2:T(8,128)(2,1)S(1)} %copy-done.3), kind=kOutput, calls=%fused_computation.16 | convolution fusion | flops 342939648 | bytes 1275416 | tf_op jit(solution)/shard_map/conv_general_dilated | solution.py:28
  48.7 1.6 %slice_convert_fusion = f32[8,32,1,16,32]{4,1,3,0,2:T(8,128)} fusion(bf16[8,32,1,24,32]{4,1,3,0,2:T(8,128)(2,1)S(1)} %bitcast.83), kind=kLoop, calls=%fused_computation.34 | loop fusion | flops 131072 | bytes 786432 | tf_op jit(solution)/shard_map/convert_element_type | solution.py:138
  50.3 2.2 %reduce_sum.37 = f32[2,4,2,2,2,32]{5,2,1,4,3,0:T(2,128)S(1)} reduce(f32[2,4,4,2,4,2,2,4,32]{8,4,3,2,7,6,5,1,0:T(4,128)} %bitcast.85, f32[]{:T(128)} %constant.12.clone.1), dimensions={1,4,7}, to_apply=%region_0.1 | reduce | flops 129024 | bytes 532484 | tf_op jit(solution)/shard_map/reduce_sum | solution.py:46
  54.0 9.3 %all_to_all.33 = bf16[4,2,768]{2,1,0:T(2,128)(2,1)S(1)} all-to-all(bf16[4,2,768]{2,1,0:T(2,128)(2,1)S(1)} %reshape.145), channel_id=1, replica_groups=mesh['gx'=4,'gy'=2,'gz'=4] {'gz'}, dimensions={0} | all-to-all | bytes 24576 | tf_op jit(solution)/shard_map/all_to_all | solution.py:124
  63.5 9.6 %all_gather.3 = bf16[2,2,256,32]{3,1,0,2:T(2,128)(2,1)S(1)} all-gather(bf16[2,2,32,32]{3,1,0,2:T(2,128)(2,1)S(1)} %copy.118), channel_id=1, replica_groups=mesh['gx'=4,'gy'=2,'gz'=4] {'gx','gy'}, dimensions={2}, use_global_device_ids=true | all-gather | bytes 73728 | tf_op jit(solution)/shard_map/all_gather | solution.py:129
  74.1 7.9 %all_to_all.34 = bf16[4,2,256]{2,1,0:T(2,128)(2,1)S(1)} all-to-all(bf16[4,2,256]{2,1,0:T(2,128)(2,1)S(1)} %reshape.147), channel_id=1, replica_groups=mesh['gx'=4,'gy'=2,'gz'=4] {'gz'}, dimensions={0} | all-to-all | bytes 8192 | tf_op jit(solution)/shard_map/all_to_all | solution.py:131
  83.5 2.2 %collective-permute-start.6 = (bf16[1,32,16,32]{3,1,2,0:T(8,128)(2,1)S(1)}, bf16[1,32,16,32]{3,1,2,0:T(8,128)(2,1)S(1)}, u32[]{:S(2)}, u32[]{:S(2)}) collective-permute-start(bf16[1,32,16,32]{3,1,2,0:T(8,128)(2,1)S(1)} %get-tuple-element.34), channel_id=1, source_target_pairs={{0,8},{8,16},{16,24},{1,9},{9,17},{17,25},{2,10},{10,18},{18,26},{... | collective-permute-start | bytes 98312 | tf_op jit(solution)/shard_map/ppermute | solution.py:18
  88.2 4.7 %collective-permute-done.7 = bf16[1,32,16,32]{3,1,2,0:T(8,128)(2,1)S(1)} collective-permute-done((bf16[1,32,16,32]{3,1,2,0:T(8,128)(2,1)S(1)}, bf16[1,32,16,32]{3,1,2,0:T(8,128)(2,1)S(1)}, u32[]{:S(2)}, u32[]{:S(2)}) %collective-permute-start.7) | collective-permute-done | bytes 32800 | tf_op jit(solution)/shard_map/ppermute | solution.py:20
  95.7 1.9 %collective-permute-done.9 = bf16[10,1,16,32]{3,1,2,0:T(2,128)(2,1)S(1)} collective-permute-done((bf16[10,1,16,32]{3,1,2,0:T(2,128)(2,1)S(1)}, bf16[10,1,16,32]{3,1,2,0:T(2,128)(2,1)S(1)}, u32[]{:S(2)}, u32[]{:S(2)}) %collective-permute-start.9) | collective-permute-done | bytes 10272 | tf_op jit(solution)/shard_map/ppermute | solution.py:20
  97.6 2.5 %collective-permute-start.10 = (bf16[10,34,1,32]{3,1,2,0:T(8,128)(2,1)S(1)}, bf16[10,34,1,32]{3,1,2,0:T(8,128)(2,1)S(1)}, u32[]{:S(2)}, u32[]{:S(2)}) collective-permute-start(bf16[10,34,1,32]{3,1,2,0:T(8,128)(2,1)S(1)} %get-tuple-element.19), channel_id=1, source_target_pairs={{0,1},{1,2},{2,3},{4,5},{5,6},{6,7},{8,9},{9,10},{10,11},{12,13},{... | collective-permute-start | bytes 65288 | tf_op jit(solution)/shard_map/ppermute | solution.py:18
  100.1 1.5 %collective-permute-start.11 = (bf16[10,34,1,32]{3,1,2,0:T(8,128)(2,1)S(1)}, bf16[10,34,1,32]{3,1,2,0:T(8,128)(2,1)S(1)}, u32[]{:S(2)}, u32[]{:S(2)}) collective-permute-start(bf16[10,34,1,32]{3,1,2,0:T(8,128)(2,1)S(1)} %get-tuple-element.20), channel_id=1, source_target_pairs={{1,0},{2,1},{3,2},{5,4},{6,5},{7,6},{9,8},{10,9},{11,10},{13,12},{... | collective-permute-start | bytes 65288 | tf_op jit(solution)/shard_map/ppermute | solution.py:20
  102.6 4.1 %collective-permute-done.11 = bf16[10,34,1,32]{3,1,2,0:T(8,128)(2,1)S(1)} collective-permute-done((bf16[10,34,1,32]{3,1,2,0:T(8,128)(2,1)S(1)}, bf16[10,34,1,32]{3,1,2,0:T(8,128)(2,1)S(1)}, u32[]{:S(2)}, u32[]{:S(2)}) %collective-permute-start.11) | collective-permute-done | bytes 21792 | tf_op jit(solution)/shard_map/ppermute | solution.py:20
  106.7 2.1 %maximum_bitcast_fusion = bf16[10,34,1,18,32]{4,1,3,0,2:T(8,128)(2,1)S(1)} fusion(bf16[10,34,1,32]{3,1,2,0:T(8,128)(2,1)S(1)} %collective-permute-done.11, bf16[10,1,16,32]{3,1,2,0:T(2,128)(2,1)S(1)} %collective-permute-done.9, bf16[1,32,16,32]{3,1,2,0:T(8,128)(2,1)S(1)} %collective-permute-done.7, bf16[8,32,16,32]{3,1,2,0:T(8,128)(2,1)S(1)} %fusion.16, ...), kind=kLoop, calls=%fused_computation.19 | loop fusion | flops 2741760 | bytes 783360 | tf_op jit(solution)/shard_map/broadcast_in_dim | solution.py:29
  108.8 2.6 %copy.133 = bf16[10,34,1,18,32]{1,4,3,2,0:T(8,128)(2,1)} copy(bf16[10,34,1,18,32]{4,1,3,0,2:T(8,128)(2,1)S(1)} %maximum_bitcast_fusion) | data formatting | bytes 783360
  111.3 1.8 %pad.2.clone = bf16[10,34,1,24,32]{1,4,3,2,0:T(8,128)(2,1)S(1)} pad(bf16[10,34,1,18,32]{1,4,3,2,0:T(8,128)(2,1)} %copy.133, bf16[]{:T(256)} %constant.34), padding=0_0x0_0x0_0x0_6x0_0 | pad | bytes 913922 | tf_op jit(solution)/shard_map/broadcast_in_dim | solution.py:29
  113.1 3.1 %copy.128 = bf16[10,34,1,8,3,32]{5,3,4,1,0,2:T(8,128)(2,1)} copy(bf16[10,34,1,8,3,32]{1,5,4,3,2,0:T(8,128)(2,1)S(1)} %bitcast.87) | data formatting | bytes 1044480 | tf_op jit(solution)/shard_map/conv_general_dilated | solution.py:28
  116.3 1.9 %slice.87 = bf16[10,34,1,7,2,32]{5,3,4,1,0,2:T(8,128)(2,1)S(1)} slice(bf16[10,34,1,8,3,32]{5,3,4,1,0,2:T(8,128)(2,1)} %copy.128), slice={[0:10], [0:34], [0:1], [1:8], [0:2], [0:32]} | slice | bytes 609280 | tf_op jit(solution)/shard_map/conv_general_dilated | solution.py:28
  118.3 4.3 %select_convert_fusion = bf16[8,32,8,3,32]{4,2,3,1,0:T(8,128)(2,1)S(1)} fusion(pred[8,3]{0,1:T(4,128)(4,1)S(1)} %copy-done.10, bf16[3,3,3,32,32]{4,3,2,1,0:T(8,128)(2,1)S(1)} %copy-done.7, bf16[10,34,1,7,2,32]{5,3,4,1,0,2:T(8,128)(2,1)S(1)} %slice.87, bf16[10,34,1,8,3,32]{5,3,4,1,0,2:T(8,128)(2,1)S(1)} %copy-done.2), kind=kOutput, calls=%fused_computation.15 | convolution fusion | flops 342743040 | bytes 1275416 | tf_op jit(solution)/shard_map/conv_general_dilated | solution.py:28
  123.0 1.4 %copy.130 = bf16[8,32,16,32]{3,2,1,0:T(8,128)(2,1)} copy(bf16[8,32,16,32]{3,1,2,0:T(8,128)(2,1)S(1)} %slice_bitcast_fusion) | data formatting | bytes 524288 | tf_op jit(solution)/shard_map/convert_element_type | solution.py:140
  (87 shorter events, 20.6 us)
Async XLA Ops:
  0.0 53.6 %copy-start = (bf16[256,512]{1,0:T(8,128)(2,1)S(1)}, bf16[256,512]{1,0:T(8,128)(2,1)}, u32[]{:S(2)}) copy-start(bf16[256,512]{1,0:T(8,128)(2,1)} %param.13) | copy-start | bytes 786436
  2.0 7.6 %collective-permute-start = (bf16[1,32,16,32]{1,3,2,0:T(8,128)(2,1)S(1)}, bf16[1,32,16,32]{1,3,2,0:T(8,128)(2,1)S(1)}, u32[]{:S(2)}, u32[]{:S(2)}) collective-permute-start(bf16[1,32,16,32]{1,3,2,0:T(8,128)(2,1)S(1)} %get-tuple-element.36), channel_id=1, source_target_pairs={{0,8},{8,16},{16,24},{1,9},{9,17},{17,25},{2,10},{10,18},{18,26},{... | collective-permute-start | bytes 98312 | tf_op jit(solution)/shard_map/ppermute | solution.py:18
  6.9 7.5 %collective-permute-start.1 = (bf16[1,32,16,32]{1,3,2,0:T(8,128)(2,1)S(1)}, bf16[1,32,16,32]{1,3,2,0:T(8,128)(2,1)S(1)}, u32[]{:S(2)}, u32[]{:S(2)}) collective-permute-start(bf16[1,32,16,32]{1,3,2,0:T(8,128)(2,1)S(1)} %get-tuple-element.37), channel_id=1, source_target_pairs={{8,0},{16,8},{24,16},{9,1},{17,9},{25,17},{10,2},{18,10},{26,18},{... | collective-permute-start | bytes 98312 | tf_op jit(solution)/shard_map/ppermute | solution.py:20
  18.7 3.6 %collective-permute-start.2 = (bf16[10,1,16,32]{3,2,1,0:T(8,128)(2,1)S(1)}, bf16[10,1,16,32]{3,2,1,0:T(8,128)(2,1)S(1)}, u32[]{:S(2)}, u32[]{:S(2)}) collective-permute-start(bf16[10,1,16,32]{3,2,1,0:T(8,128)(2,1)S(1)} %copy.104), channel_id=1, source_target_pairs={{0,4},{1,5},{2,6},{3,7},{8,12},{9,13},{10,14},{11,15},{16,20},{17,... | collective-permute-start | bytes 30728 | tf_op jit(solution)/shard_map/ppermute | solution.py:18
  21.0 3.1 %collective-permute-start.3 = (bf16[10,1,16,32]{3,2,1,0:T(8,128)(2,1)S(1)}, bf16[10,1,16,32]{3,2,1,0:T(8,128)(2,1)S(1)}, u32[]{:S(2)}, u32[]{:S(2)}) collective-permute-start(bf16[10,1,16,32]{3,2,1,0:T(8,128)(2,1)S(1)} %copy.105), channel_id=1, source_target_pairs={{4,0},{5,1},{6,2},{7,3},{12,8},{13,9},{14,10},{15,11},{20,16},{21,... | collective-permute-start | bytes 30728 | tf_op jit(solution)/shard_map/ppermute | solution.py:20
  26.2 11.0 %copy-start.1 = (bf16[10,1,16,32]{1,3,2,0:T(8,128)(2,1)S(1)}, bf16[10,1,16,32]{1,3,2,0:T(8,128)(2,1)}, u32[]{:S(2)}) copy-start(bf16[10,1,16,32]{1,3,2,0:T(8,128)(2,1)} %copy.107) | copy-start | bytes 30724
  27.4 5.7 %collective-permute-start.4 = (bf16[10,34,1,32]{1,3,2,0:T(8,128)(2,1)S(1)}, bf16[10,34,1,32]{1,3,2,0:T(8,128)(2,1)S(1)}, u32[]{:S(2)}, u32[]{:S(2)}) collective-permute-start(bf16[10,34,1,32]{1,3,2,0:T(8,128)(2,1)S(1)} %get-tuple-element.17), channel_id=1, source_target_pairs={{0,1},{1,2},{2,3},{4,5},{5,6},{6,7},{8,9},{9,10},{10,11},{12,13},{... | collective-permute-start | bytes 65288 | tf_op jit(solution)/shard_map/ppermute | solution.py:18
  30.9 6.3 %collective-permute-start.5 = (bf16[10,34,1,32]{1,3,2,0:T(8,128)(2,1)S(1)}, bf16[10,34,1,32]{1,3,2,0:T(8,128)(2,1)S(1)}, u32[]{:S(2)}, u32[]{:S(2)}) collective-permute-start(bf16[10,34,1,32]{1,3,2,0:T(8,128)(2,1)S(1)} %get-tuple-element.18), channel_id=1, source_target_pairs={{1,0},{2,1},{3,2},{5,4},{6,5},{7,6},{9,8},{10,9},{11,10},{13,12},{... | collective-permute-start | bytes 65288 | tf_op jit(solution)/shard_map/ppermute | solution.py:20
  42.0 2.0 %copy-start.3 = (bf16[10,34,1,8,3,32]{5,3,4,1,0,2:T(8,128)(2,1)S(1)}, bf16[10,34,1,8,3,32]{5,3,4,1,0,2:T(8,128)(2,1)}, u32[]{:S(2)}) copy-start(bf16[10,34,1,8,3,32]{5,3,4,1,0,2:T(8,128)(2,1)} %copy.109) | copy-start | bytes 1566724
  42.0 2.0 %copy-start.6 = (bf16[3,3,3,32,32]{4,3,2,1,0:T(8,128)(2,1)S(1)}, bf16[3,3,3,32,32]{4,3,2,1,0:T(8,128)(2,1)}, u32[]{:S(2)}) copy-start(bf16[3,3,3,32,32]{4,3,2,1,0:T(8,128)(2,1)} %param.9) | copy-start | bytes 165892
  42.0 2.0 %copy-start.10 = (pred[8,3]{0,1:T(4,128)(4,1)S(1)}, pred[8,3]{0,1:T(4,128)(4,1)}, u32[]{:S(2)}) copy-start(pred[8,3]{0,1:T(4,128)(4,1)} %constant.42) | copy-start | bytes 76
  48.7 4.7 %copy-start.8 = (bf16[256,256]{1,0:T(8,128)(2,1)S(1)}, bf16[256,256]{1,0:T(8,128)(2,1)}, u32[]{:S(2)}) copy-start(bf16[256,256]{1,0:T(8,128)(2,1)} %param.12) | copy-start | bytes 393220
  48.7 4.7 %copy-start.9 = (f32[256]{0:T(256)S(1)}, f32[256]{0:T(256)}, u32[]{:S(2)}) copy-start(f32[256]{0:T(256)} %param.11) | copy-start | bytes 3076
  50.3 31.9 %copy-start.4 = (bf16[256,256]{1,0:T(8,128)(2,1)S(1)}, bf16[256,256]{1,0:T(8,128)(2,1)}, u32[]{:S(2)}) copy-start(bf16[256,256]{1,0:T(8,128)(2,1)} %param.15) | copy-start | bytes 393220
  50.3 31.9 %copy-start.5 = (bf16[256,256]{1,0:T(8,128)(2,1)S(1)}, bf16[256,256]{1,0:T(8,128)(2,1)}, u32[]{:S(2)}) copy-start(bf16[256,256]{1,0:T(8,128)(2,1)} %param.14) | copy-start | bytes 393220
  83.5 4.7 %collective-permute-start.6 = (bf16[1,32,16,32]{3,1,2,0:T(8,128)(2,1)S(1)}, bf16[1,32,16,32]{3,1,2,0:T(8,128)(2,1)S(1)}, u32[]{:S(2)}, u32[]{:S(2)}) collective-permute-start(bf16[1,32,16,32]{3,1,2,0:T(8,128)(2,1)S(1)} %get-tuple-element.34), channel_id=1, source_target_pairs={{0,8},{8,16},{16,24},{1,9},{9,17},{17,25},{2,10},{10,18},{18,26},{... | collective-permute-start | bytes 98312 | tf_op jit(solution)/shard_map/ppermute | solution.py:18
  85.7 7.2 %collective-permute-start.7 = (bf16[1,32,16,32]{3,1,2,0:T(8,128)(2,1)S(1)}, bf16[1,32,16,32]{3,1,2,0:T(8,128)(2,1)S(1)}, u32[]{:S(2)}, u32[]{:S(2)}) collective-permute-start(bf16[1,32,16,32]{3,1,2,0:T(8,128)(2,1)S(1)} %get-tuple-element.35), channel_id=1, source_target_pairs={{8,0},{16,8},{24,16},{9,1},{17,9},{25,17},{10,2},{18,10},{26,18},{... | collective-permute-start | bytes 98312 | tf_op jit(solution)/shard_map/ppermute | solution.py:20
  93.1 2.6 %collective-permute-start.8 = (bf16[10,1,16,32]{3,1,2,0:T(2,128)(2,1)S(1)}, bf16[10,1,16,32]{3,1,2,0:T(2,128)(2,1)S(1)}, u32[]{:S(2)}, u32[]{:S(2)}) collective-permute-start(bf16[10,1,16,32]{3,1,2,0:T(2,128)(2,1)S(1)} %get-tuple-element.28), channel_id=1, source_target_pairs={{0,4},{1,5},{2,6},{3,7},{8,12},{9,13},{10,14},{11,15},{16,20},{17,... | collective-permute-start | bytes 30728 | tf_op jit(solution)/shard_map/ppermute | solution.py:18
  94.4 3.2 %collective-permute-start.9 = (bf16[10,1,16,32]{3,1,2,0:T(2,128)(2,1)S(1)}, bf16[10,1,16,32]{3,1,2,0:T(2,128)(2,1)S(1)}, u32[]{:S(2)}, u32[]{:S(2)}) collective-permute-start(bf16[10,1,16,32]{3,1,2,0:T(2,128)(2,1)S(1)} %get-tuple-element.30), channel_id=1, source_target_pairs={{4,0},{5,1},{6,2},{7,3},{12,8},{13,9},{14,10},{15,11},{20,16},{21,... | collective-permute-start | bytes 30728 | tf_op jit(solution)/shard_map/ppermute | solution.py:20
  97.6 4.9 %collective-permute-start.10 = (bf16[10,34,1,32]{3,1,2,0:T(8,128)(2,1)S(1)}, bf16[10,34,1,32]{3,1,2,0:T(8,128)(2,1)S(1)}, u32[]{:S(2)}, u32[]{:S(2)}) collective-permute-start(bf16[10,34,1,32]{3,1,2,0:T(8,128)(2,1)S(1)} %get-tuple-element.19), channel_id=1, source_target_pairs={{0,1},{1,2},{2,3},{4,5},{5,6},{6,7},{8,9},{9,10},{10,11},{12,13},{... | collective-permute-start | bytes 65288 | tf_op jit(solution)/shard_map/ppermute | solution.py:18
  100.1 6.6 %collective-permute-start.11 = (bf16[10,34,1,32]{3,1,2,0:T(8,128)(2,1)S(1)}, bf16[10,34,1,32]{3,1,2,0:T(8,128)(2,1)S(1)}, u32[]{:S(2)}, u32[]{:S(2)}) collective-permute-start(bf16[10,34,1,32]{3,1,2,0:T(8,128)(2,1)S(1)} %get-tuple-element.20), channel_id=1, source_target_pairs={{1,0},{2,1},{3,2},{5,4},{6,5},{7,6},{9,8},{10,9},{11,10},{13,12},{... | collective-permute-start | bytes 65288 | tf_op jit(solution)/shard_map/ppermute | solution.py:20
  116.3 2.0 %copy-start.2 = (bf16[10,34,1,8,3,32]{5,3,4,1,0,2:T(8,128)(2,1)S(1)}, bf16[10,34,1,8,3,32]{5,3,4,1,0,2:T(8,128)(2,1)}, u32[]{:S(2)}) copy-start(bf16[10,34,1,8,3,32]{5,3,4,1,0,2:T(8,128)(2,1)} %copy.128) | copy-start | bytes 1566724
  116.3 2.0 %copy-start.7 = (bf16[3,3,3,32,32]{4,3,2,1,0:T(8,128)(2,1)S(1)}, bf16[3,3,3,32,32]{4,3,2,1,0:T(8,128)(2,1)}, u32[]{:S(2)}) copy-start(bf16[3,3,3,32,32]{4,3,2,1,0:T(8,128)(2,1)} %param.10) | copy-start | bytes 165892
where the time goes:
time: 125 us; the launch traced here: 124 us
  local copies, waits for them, and re-layouts  29.4 us (24%)
  blocking collectives  26.7 us (21%)
  waiting for transfers between devices  24.6 us (20%)
  starting transfers between devices  23.8 us (19%)
  matrix products  9.77 us (8%)
  other arithmetic  9.75 us (8%)
    ppermute x6, waiting for transfers between devices, with_halo(): lax.ppermute(head, axis, [((i + 1) % count, i) for i in range(ends)])  20.3 us
    ppermute x6, starting transfers between devices, with_halo(): lax.ppermute(tail, axis, [(i, (i + 1) % count) for i in range(ends)])  15.6 us
    conv_general_dilated x4, local copies, waits for them, and re-layouts, convolve(): lax.conv_general_dilated(padded[None], kernel, (1, 1, 1), 'VALID', dimens...  9.95 us
    all_gather x1, blocking collectives, on_device(): lax.all_gather(arranged[1:], ('gx', 'gy'), axis=2, tiled=True)  9.56 us
    all_to_all x1, blocking collectives, on_device(): lax.all_to_all(packed, 'gz', split_axis=1, concat_axis=2, tiled=True)  9.26 us
    conv_general_dilated x2, matrix products, convolve(): lax.conv_general_dilated(padded[None], kernel, (1, 1, 1), 'VALID', dimens...  8.72 us
    ppermute x6, starting transfers between devices, with_halo(): lax.ppermute(head, axis, [((i + 1) % count, i) for i in range(ends)])  8.15 us
    all_to_all x1, blocking collectives, on_device(): lax.all_to_all(finish(running), 'gz', split_axis=1, concat_axis=0, tiled=...  7.91 us
  transfers between devices with their start and end apart: 12, of which 10 were waited for; matrix products, arithmetic and copies ran while one was open for 2% of the time, Pallas kernels for 0%

commit v1 on v0

--- a/solution.py
+++ b/solution.py
@@ -128,7 +128,12 @@
         start_state(head_queries),
         lax.all_gather(arranged[1:], ("gx", "gy"), axis=2, tiled=True),
     )
-    returned = lax.all_to_all(finish(running), "gz", split_axis=1, concat_axis=0, tiled=True)
+    returned = jnp.concatenate(
+        lax.all_to_all(
+            jnp.stack(jnp.split(finish(running), lax.axis_size("gz"), axis=1)), "gz", 0, 0
+        ),
+        axis=0,
+    )
     attended = returned.transpose(1, 0, 2).reshape(token_count, width)
     mixture = (tokens + jnp.dot(attended, out_weight, preferred_element_type=jnp.float32)).astype(
         jnp.bfloat16

time: 125 us -> 125 us (level)
  no operation moved by 1% of the time
where the time goes in v1:
time: 125 us; the launch traced here: 124 us
  local copies, waits for them, and re-layouts  29.3 us (23%)
  blocking collectives  26.7 us (21%)
  waiting for transfers between devices  24.6 us (20%)
  starting transfers between devices  23.8 us (19%)
  matrix products  9.77 us (8%)
  other arithmetic  9.75 us (8%)
    ppermute x6, waiting for transfers between devices, with_halo(): lax.ppermute(head, axis, [((i + 1) % count, i) for i in range(ends)])  20.3 us
    ppermute x6, starting transfers between devices, with_halo(): lax.ppermute(tail, axis, [(i, (i + 1) % count) for i in range(ends)])  15.6 us
    conv_general_dilated x4, local copies, waits for them, and re-layouts, convolve(): lax.conv_general_dilated(padded[None], kernel, (1, 1, 1), 'VALID', dimens...  9.9 us
    all_gather x1, blocking collectives, on_device(): lax.all_gather(arranged[1:], ('gx', 'gy'), axis=2, tiled=True)  9.56 us
    all_to_all x1, blocking collectives, on_device(): lax.all_to_all(packed, 'gz', split_axis=1, concat_axis=2, tiled=True)  9.26 us
    conv_general_dilated x2, matrix products, convolve(): lax.conv_general_dilated(padded[None], kernel, (1, 1, 1), 'VALID', dimens...  8.72 us
    ppermute x6, starting transfers between devices, with_halo(): lax.ppermute(head, axis, [((i + 1) % count, i) for i in range(ends)])  8.15 us
    all_to_all x1, blocking collectives, on_device(): lax.all_to_all(jnp.stack(jnp.split(finish(running), lax.axis_size('gz'),...  7.91 us
  transfers between devices with their start and end apart: 12, of which 10 were waited for; matrix products, arithmetic and copies ran while one was open for 2% of the time, Pallas kernels for 0%

profile of v1, /device:TPU:0, one launch (start us, length us, event | category | flops | bytes accessed | tf_op | source)
XLA Modules:
  0.0 124.3 jit_solution(3559177864279818619)
XLA Ops:
  0.0 2.0 %copy.69 = bf16[8,32,16,32]{1,3,2,0:T(8,128)(2,1)S(1)} copy(bf16[8,32,16,32]{3,2,1,0:T(8,128)(2,1)} %param.8) | data formatting | bytes 524288 | tf_op args[0]
  2.0 4.9 %collective-permute-start = (bf16[1,32,16,32]{1,3,2,0:T(8,128)(2,1)S(1)}, bf16[1,32,16,32]{1,3,2,0:T(8,128)(2,1)S(1)}, u32[]{:S(2)}, u32[]{:S(2)}) collective-permute-start(bf16[1,32,16,32]{1,3,2,0:T(8,128)(2,1)S(1)} %get-tuple-element.36), channel_id=1, source_target_pairs={{0,8},{8,16},{16,24},{1,9},{9,17},{17,25},{2,10},{10,18},{18,26},{... | collective-permute-start | bytes 98312 | tf_op jit(solution)/shard_map/ppermute | solution.py:18
  8.2 1.4 %collective-permute-done = bf16[1,32,16,32]{1,3,2,0:T(8,128)(2,1)S(1)} collective-permute-done((bf16[1,32,16,32]{1,3,2,0:T(8,128)(2,1)S(1)}, bf16[1,32,16,32]{1,3,2,0:T(8,128)(2,1)S(1)}, u32[]{:S(2)}, u32[]{:S(2)}) %collective-permute-start) | collective-permute-done | bytes 32800 | tf_op jit(solution)/shard_map/ppermute | solution.py:18
  9.6 4.8 %collective-permute-done.1 = bf16[1,32,16,32]{1,3,2,0:T(8,128)(2,1)S(1)} collective-permute-done((bf16[1,32,16,32]{1,3,2,0:T(8,128)(2,1)S(1)}, bf16[1,32,16,32]{1,3,2,0:T(8,128)(2,1)S(1)}, u32[]{:S(2)}, u32[]{:S(2)}) %collective-permute-start.1) | collective-permute-done | bytes 32800 | tf_op jit(solution)/shard_map/ppermute | solution.py:20
  14.7 1.7 %fusion.43 = (bf16[10,1,16,32]{1,3,2,0:T(8,128)(2,1)}, bf16[10,1,16,32]{1,3,2,0:T(8,128)(2,1)S(1)}) fusion(bf16[10,32,16,32]{1,3,2,0:T(8,128)(2,1)S(1)} %pad_maximum_fusion), kind=kLoop, calls=%fused_computation.80 | loop fusion | bytes 40960 | tf_op jit(solution)/shard_map/slice | solution.py:15
  16.4 2.3 %copy.72 = bf16[10,1,16,32]{3,2,1,0:T(8,128)(2,1)S(1)} copy(bf16[10,1,16,32]{1,3,2,0:T(8,128)(2,1)} %get-tuple-element.32) | data formatting | bytes 20480 | tf_op jit(solution)/shard_map/slice | solution.py:15
  18.7 1.3 %collective-permute-start.2 = (bf16[10,1,16,32]{3,2,1,0:T(8,128)(2,1)S(1)}, bf16[10,1,16,32]{3,2,1,0:T(8,128)(2,1)S(1)}, u32[]{:S(2)}, u32[]{:S(2)}) collective-permute-start(bf16[10,1,16,32]{3,2,1,0:T(8,128)(2,1)S(1)} %copy.72), channel_id=1, source_target_pairs={{0,4},{1,5},{2,6},{3,7},{8,12},{9,13},{10,14},{11,15},{16,20},{17,... | collective-permute-start | bytes 30728 | tf_op jit(solution)/shard_map/ppermute | solution.py:18
  24.1 2.1 %copy.75 = bf16[10,1,16,32]{1,3,2,0:T(8,128)(2,1)} copy(bf16[10,1,16,32]{3,2,1,0:T(8,128)(2,1)S(1)} %collective-permute-done.3) | data formatting | bytes 20480 | tf_op jit(solution)/shard_map/ppermute | solution.py:20
  27.4 3.5 %collective-permute-start.4 = (bf16[10,34,1,32]{1,3,2,0:T(8,128)(2,1)S(1)}, bf16[10,34,1,32]{1,3,2,0:T(8,128)(2,1)S(1)}, u32[]{:S(2)}, u32[]{:S(2)}) collective-permute-start(bf16[10,34,1,32]{1,3,2,0:T(8,128)(2,1)S(1)} %get-tuple-element.17), channel_id=1, source_target_pairs={{0,1},{1,2},{2,3},{4,5},{5,6},{6,7},{8,9},{9,10},{10,11},{12,13},{... | collective-permute-start | bytes 65288 | tf_op jit(solution)/shard_map/ppermute | solution.py:18
  30.9 1.5 %collective-permute-start.5 = (bf16[10,34,1,32]{1,3,2,0:T(8,128)(2,1)S(1)}, bf16[10,34,1,32]{1,3,2,0:T(8,128)(2,1)S(1)}, u32[]{:S(2)}, u32[]{:S(2)}) collective-permute-start(bf16[10,34,1,32]{1,3,2,0:T(8,128)(2,1)S(1)} %get-tuple-element.18), channel_id=1, source_target_pairs={{1,0},{2,1},{3,2},{5,4},{6,5},{7,6},{9,8},{10,9},{11,10},{13,12},{... | collective-permute-start | bytes 65288 | tf_op jit(solution)/shard_map/ppermute | solution.py:20
  33.2 4.1 %collective-permute-done.5 = bf16[10,34,1,32]{1,3,2,0:T(8,128)(2,1)S(1)} collective-permute-done((bf16[10,34,1,32]{1,3,2,0:T(8,128)(2,1)S(1)}, bf16[10,34,1,32]{1,3,2,0:T(8,128)(2,1)S(1)}, u32[]{:S(2)}, u32[]{:S(2)}) %collective-permute-start.5) | collective-permute-done | bytes 21792 | tf_op jit(solution)/shard_map/ppermute | solution.py:20
  38.9 3.1 %copy.77 = bf16[10,34,1,8,3,32]{5,3,4,1,0,2:T(8,128)(2,1)} copy(bf16[10,34,1,8,3,32]{1,5,4,3,2,0:T(8,128)(2,1)S(1)} %bitcast.88) | data formatting | bytes 1044480 | tf_op jit(solution)/shard_map/conv_general_dilated | solution.py:28
  42.0 1.9 %slice.79 = bf16[10,34,1,7,2,32]{5,3,4,1,0,2:T(8,128)(2,1)S(1)} slice(bf16[10,34,1,8,3,32]{5,3,4,1,0,2:T(8,128)(2,1)} %copy.77), slice={[0:10], [0:34], [0:1], [1:8], [0:2], [0:32]} | slice | bytes 609280 | tf_op jit(solution)/shard_map/conv_general_dilated | solution.py:28
  44.0 4.4 %maximum_convert_fusion = bf16[8,32,8,3,32]{4,2,3,1,0:T(8,128)(2,1)S(1)} fusion(pred[8,3]{0,1:T(4,128)(4,1)S(1)} %copy-done.10, bf16[3,3,3,32,32]{4,3,2,1,0:T(8,128)(2,1)S(1)} %copy-done.6, bf16[10,34,1,7,2,32]{5,3,4,1,0,2:T(8,128)(2,1)S(1)} %slice.79, bf16[10,34,1,8,3,32]{5,3,4,1,0,2:T(8,128)(2,1)S(1)} %copy-done.3), kind=kOutput, calls=%fused_computation.16 | convolution fusion | flops 342939648 | bytes 1275416 | tf_op jit(solution)/shard_map/conv_general_dilated | solution.py:28
  48.7 1.6 %slice_convert_fusion = f32[8,32,1,16,32]{4,1,3,0,2:T(8,128)} fusion(bf16[8,32,1,24,32]{4,1,3,0,2:T(8,128)(2,1)S(1)} %bitcast.83), kind=kLoop, calls=%fused_computation.34 | loop fusion | flops 131072 | bytes 786432 | tf_op jit(solution)/shard_map/convert_element_type | solution.py:143
  50.3 2.2 %reduce_sum.37 = f32[2,4,2,2,2,32]{5,2,1,4,3,0:T(2,128)S(1)} reduce(f32[2,4,4,2,4,2,2,4,32]{8,4,3,2,7,6,5,1,0:T(4,128)} %bitcast.85, f32[]{:T(128)} %constant.12.clone.1), dimensions={1,4,7}, to_apply=%region_0.1 | reduce | flops 129024 | bytes 532484 | tf_op jit(solution)/shard_map/reduce_sum | solution.py:46
  54.0 9.3 %all_to_all.20 = bf16[4,2,768]{2,1,0:T(2,128)(2,1)S(1)} all-to-all(bf16[4,2,768]{2,1,0:T(2,128)(2,1)S(1)} %reshape.149), channel_id=1, replica_groups=mesh['gx'=4,'gy'=2,'gz'=4] {'gz'}, dimensions={0} | all-to-all | bytes 24576 | tf_op jit(solution)/shard_map/all_to_all | solution.py:124
  63.5 9.6 %all_gather.3 = bf16[2,2,256,32]{3,1,0,2:T(2,128)(2,1)S(1)} all-gather(bf16[2,2,32,32]{3,1,0,2:T(2,128)(2,1)S(1)} %copy.86), channel_id=1, replica_groups=mesh['gx'=4,'gy'=2,'gz'=4] {'gx','gy'}, dimensions={2}, use_global_device_ids=true | all-gather | bytes 73728 | tf_op jit(solution)/shard_map/all_gather | solution.py:129
  74.1 7.9 %all_to_all.21 = bf16[4,2,256]{2,1,0:T(2,128)(2,1)S(1)} all-to-all(bf16[4,2,256]{2,1,0:T(2,128)(2,1)S(1)} %reshape.151), channel_id=1, replica_groups=mesh['gx'=4,'gy'=2,'gz'=4] {'gz'}, dimensions={0} | all-to-all | bytes 8192 | tf_op jit(solution)/shard_map/all_to_all | solution.py:132
  83.5 2.2 %collective-permute-start.6 = (bf16[1,32,16,32]{3,1,2,0:T(8,128)(2,1)S(1)}, bf16[1,32,16,32]{3,1,2,0:T(8,128)(2,1)S(1)}, u32[]{:S(2)}, u32[]{:S(2)}) collective-permute-start(bf16[1,32,16,32]{3,1,2,0:T(8,128)(2,1)S(1)} %get-tuple-element.34), channel_id=1, source_target_pairs={{0,8},{8,16},{16,24},{1,9},{9,17},{17,25},{2,10},{10,18},{18,26},{... | collective-permute-start | bytes 98312 | tf_op jit(solution)/shard_map/ppermute | solution.py:18
  88.2 4.7 %collective-permute-done.7 = bf16[1,32,16,32]{3,1,2,0:T(8,128)(2,1)S(1)} collective-permute-done((bf16[1,32,16,32]{3,1,2,0:T(8,128)(2,1)S(1)}, bf16[1,32,16,32]{3,1,2,0:T(8,128)(2,1)S(1)}, u32[]{:S(2)}, u32[]{:S(2)}) %collective-permute-start.7) | collective-permute-done | bytes 32800 | tf_op jit(solution)/shard_map/ppermute | solution.py:20
  95.6 1.9 %collective-permute-done.9 = bf16[10,1,16,32]{3,1,2,0:T(2,128)(2,1)S(1)} collective-permute-done((bf16[10,1,16,32]{3,1,2,0:T(2,128)(2,1)S(1)}, bf16[10,1,16,32]{3,1,2,0:T(2,128)(2,1)S(1)}, u32[]{:S(2)}, u32[]{:S(2)}) %collective-permute-start.9) | collective-permute-done | bytes 10272 | tf_op jit(solution)/shard_map/ppermute | solution.py:20
  97.6 2.5 %collective-permute-start.10 = (bf16[10,34,1,32]{3,1,2,0:T(8,128)(2,1)S(1)}, bf16[10,34,1,32]{3,1,2,0:T(8,128)(2,1)S(1)}, u32[]{:S(2)}, u32[]{:S(2)}) collective-permute-start(bf16[10,34,1,32]{3,1,2,0:T(8,128)(2,1)S(1)} %get-tuple-element.19), channel_id=1, source_target_pairs={{0,1},{1,2},{2,3},{4,5},{5,6},{6,7},{8,9},{9,10},{10,11},{12,13},{... | collective-permute-start | bytes 65288 | tf_op jit(solution)/shard_map/ppermute | solution.py:18
  100.1 1.5 %collective-permute-start.11 = (bf16[10,34,1,32]{3,1,2,0:T(8,128)(2,1)S(1)}, bf16[10,34,1,32]{3,1,2,0:T(8,128)(2,1)S(1)}, u32[]{:S(2)}, u32[]{:S(2)}) collective-permute-start(bf16[10,34,1,32]{3,1,2,0:T(8,128)(2,1)S(1)} %get-tuple-element.20), channel_id=1, source_target_pairs={{1,0},{2,1},{3,2},{5,4},{6,5},{7,6},{9,8},{10,9},{11,10},{13,12},{... | collective-permute-start | bytes 65288 | tf_op jit(solution)/shard_map/ppermute | solution.py:20
  102.5 4.1 %collective-permute-done.11 = bf16[10,34,1,32]{3,1,2,0:T(8,128)(2,1)S(1)} collective-permute-done((bf16[10,34,1,32]{3,1,2,0:T(8,128)(2,1)S(1)}, bf16[10,34,1,32]{3,1,2,0:T(8,128)(2,1)S(1)}, u32[]{:S(2)}, u32[]{:S(2)}) %collective-permute-start.11) | collective-permute-done | bytes 21792 | tf_op jit(solution)/shard_map/ppermute | solution.py:20
  106.7 2.1 %maximum_bitcast_fusion = bf16[10,34,1,18,32]{4,1,3,0,2:T(8,128)(2,1)S(1)} fusion(bf16[10,34,1,32]{3,1,2,0:T(8,128)(2,1)S(1)} %collective-permute-done.11, bf16[10,1,16,32]{3,1,2,0:T(2,128)(2,1)S(1)} %collective-permute-done.9, bf16[1,32,16,32]{3,1,2,0:T(8,128)(2,1)S(1)} %collective-permute-done.7, bf16[8,32,16,32]{3,1,2,0:T(8,128)(2,1)S(1)} %fusion.16, ...), kind=kLoop, calls=%fused_computation.19 | loop fusion | flops 2741760 | bytes 783360 | tf_op jit(solution)/shard_map/broadcast_in_dim | solution.py:29
  108.7 2.6 %copy.98 = bf16[10,34,1,18,32]{1,4,3,2,0:T(8,128)(2,1)} copy(bf16[10,34,1,18,32]{4,1,3,0,2:T(8,128)(2,1)S(1)} %maximum_bitcast_fusion) | data formatting | bytes 783360
  111.3 1.8 %pad.2.clone = bf16[10,34,1,24,32]{1,4,3,2,0:T(8,128)(2,1)S(1)} pad(bf16[10,34,1,18,32]{1,4,3,2,0:T(8,128)(2,1)} %copy.98, bf16[]{:T(256)} %constant.34), padding=0_0x0_0x0_0x0_6x0_0 | pad | bytes 913922 | tf_op jit(solution)/shard_map/broadcast_in_dim | solution.py:29
  113.1 3.1 %copy.93 = bf16[10,34,1,8,3,32]{5,3,4,1,0,2:T(8,128)(2,1)} copy(bf16[10,34,1,8,3,32]{1,5,4,3,2,0:T(8,128)(2,1)S(1)} %bitcast.87) | data formatting | bytes 1044480 | tf_op jit(solution)/shard_map/conv_general_dilated | solution.py:28
  116.2 1.9 %slice.87 = bf16[10,34,1,7,2,32]{5,3,4,1,0,2:T(8,128)(2,1)S(1)} slice(bf16[10,34,1,8,3,32]{5,3,4,1,0,2:T(8,128)(2,1)} %copy.93), slice={[0:10], [0:34], [0:1], [1:8], [0:2], [0:32]} | slice | bytes 609280 | tf_op jit(solution)/shard_map/conv_general_dilated | solution.py:28
  118.2 4.3 %select_convert_fusion = bf16[8,32,8,3,32]{4,2,3,1,0:T(8,128)(2,1)S(1)} fusion(pred[8,3]{0,1:T(4,128)(4,1)S(1)} %copy-done.10, bf16[3,3,3,32,32]{4,3,2,1,0:T(8,128)(2,1)S(1)} %copy-done.7, bf16[10,34,1,7,2,32]{5,3,4,1,0,2:T(8,128)(2,1)S(1)} %slice.87, bf16[10,34,1,8,3,32]{5,3,4,1,0,2:T(8,128)(2,1)S(1)} %copy-done.2), kind=kOutput, calls=%fused_computation.15 | convolution fusion | flops 342743040 | bytes 1275416 | tf_op jit(solution)/shard_map/conv_general_dilated | solution.py:28
  123.0 1.4 %copy.95 = bf16[8,32,16,32]{3,2,1,0:T(8,128)(2,1)} copy(bf16[8,32,16,32]{3,1,2,0:T(8,128)(2,1)S(1)} %slice_bitcast_fusion) | data formatting | bytes 524288 | tf_op jit(solution)/shard_map/convert_element_type | solution.py:145
  (86 shorter events, 20.6 us)
Async XLA Ops:
  0.0 53.6 %copy-start = (bf16[256,512]{1,0:T(8,128)(2,1)S(1)}, bf16[256,512]{1,0:T(8,128)(2,1)}, u32[]{:S(2)}) copy-start(bf16[256,512]{1,0:T(8,128)(2,1)} %param.13) | copy-start | bytes 786436
  2.0 7.6 %collective-permute-start = (bf16[1,32,16,32]{1,3,2,0:T(8,128)(2,1)S(1)}, bf16[1,32,16,32]{1,3,2,0:T(8,128)(2,1)S(1)}, u32[]{:S(2)}, u32[]{:S(2)}) collective-permute-start(bf16[1,32,16,32]{1,3,2,0:T(8,128)(2,1)S(1)} %get-tuple-element.36), channel_id=1, source_target_pairs={{0,8},{8,16},{16,24},{1,9},{9,17},{17,25},{2,10},{10,18},{18,26},{... | collective-permute-start | bytes 98312 | tf_op jit(solution)/shard_map/ppermute | solution.py:18
  6.9 7.5 %collective-permute-start.1 = (bf16[1,32,16,32]{1,3,2,0:T(8,128)(2,1)S(1)}, bf16[1,32,16,32]{1,3,2,0:T(8,128)(2,1)S(1)}, u32[]{:S(2)}, u32[]{:S(2)}) collective-permute-start(bf16[1,32,16,32]{1,3,2,0:T(8,128)(2,1)S(1)} %get-tuple-element.37), channel_id=1, source_target_pairs={{8,0},{16,8},{24,16},{9,1},{17,9},{25,17},{10,2},{18,10},{26,18},{... | collective-permute-start | bytes 98312 | tf_op jit(solution)/shard_map/ppermute | solution.py:20
  18.7 3.6 %collective-permute-start.2 = (bf16[10,1,16,32]{3,2,1,0:T(8,128)(2,1)S(1)}, bf16[10,1,16,32]{3,2,1,0:T(8,128)(2,1)S(1)}, u32[]{:S(2)}, u32[]{:S(2)}) collective-permute-start(bf16[10,1,16,32]{3,2,1,0:T(8,128)(2,1)S(1)} %copy.72), channel_id=1, source_target_pairs={{0,4},{1,5},{2,6},{3,7},{8,12},{9,13},{10,14},{11,15},{16,20},{17,... | collective-permute-start | bytes 30728 | tf_op jit(solution)/shard_map/ppermute | solution.py:18
  21.0 3.1 %collective-permute-start.3 = (bf16[10,1,16,32]{3,2,1,0:T(8,128)(2,1)S(1)}, bf16[10,1,16,32]{3,2,1,0:T(8,128)(2,1)S(1)}, u32[]{:S(2)}, u32[]{:S(2)}) collective-permute-start(bf16[10,1,16,32]{3,2,1,0:T(8,128)(2,1)S(1)} %copy.73), channel_id=1, source_target_pairs={{4,0},{5,1},{6,2},{7,3},{12,8},{13,9},{14,10},{15,11},{20,16},{21,... | collective-permute-start | bytes 30728 | tf_op jit(solution)/shard_map/ppermute | solution.py:20
  26.2 11.0 %copy-start.1 = (bf16[10,1,16,32]{1,3,2,0:T(8,128)(2,1)S(1)}, bf16[10,1,16,32]{1,3,2,0:T(8,128)(2,1)}, u32[]{:S(2)}) copy-start(bf16[10,1,16,32]{1,3,2,0:T(8,128)(2,1)} %copy.75) | copy-start | bytes 30724
  27.4 5.7 %collective-permute-start.4 = (bf16[10,34,1,32]{1,3,2,0:T(8,128)(2,1)S(1)}, bf16[10,34,1,32]{1,3,2,0:T(8,128)(2,1)S(1)}, u32[]{:S(2)}, u32[]{:S(2)}) collective-permute-start(bf16[10,34,1,32]{1,3,2,0:T(8,128)(2,1)S(1)} %get-tuple-element.17), channel_id=1, source_target_pairs={{0,1},{1,2},{2,3},{4,5},{5,6},{6,7},{8,9},{9,10},{10,11},{12,13},{... | collective-permute-start | bytes 65288 | tf_op jit(solution)/shard_map/ppermute | solution.py:18
  30.9 6.3 %collective-permute-start.5 = (bf16[10,34,1,32]{1,3,2,0:T(8,128)(2,1)S(1)}, bf16[10,34,1,32]{1,3,2,0:T(8,128)(2,1)S(1)}, u32[]{:S(2)}, u32[]{:S(2)}) collective-permute-start(bf16[10,34,1,32]{1,3,2,0:T(8,128)(2,1)S(1)} %get-tuple-element.18), channel_id=1, source_target_pairs={{1,0},{2,1},{3,2},{5,4},{6,5},{7,6},{9,8},{10,9},{11,10},{13,12},{... | collective-permute-start | bytes 65288 | tf_op jit(solution)/shard_map/ppermute | solution.py:20
  42.0 2.0 %copy-start.3 = (bf16[10,34,1,8,3,32]{5,3,4,1,0,2:T(8,128)(2,1)S(1)}, bf16[10,34,1,8,3,32]{5,3,4,1,0,2:T(8,128)(2,1)}, u32[]{:S(2)}) copy-start(bf16[10,34,1,8,3,32]{5,3,4,1,0,2:T(8,128)(2,1)} %copy.77) | copy-start | bytes 1566724
  42.0 2.0 %copy-start.6 = (bf16[3,3,3,32,32]{4,3,2,1,0:T(8,128)(2,1)S(1)}, bf16[3,3,3,32,32]{4,3,2,1,0:T(8,128)(2,1)}, u32[]{:S(2)}) copy-start(bf16[3,3,3,32,32]{4,3,2,1,0:T(8,128)(2,1)} %param.9) | copy-start | bytes 165892
  42.0 2.0 %copy-start.10 = (pred[8,3]{0,1:T(4,128)(4,1)S(1)}, pred[8,3]{0,1:T(4,128)(4,1)}, u32[]{:S(2)}) copy-start(pred[8,3]{0,1:T(4,128)(4,1)} %constant.42) | copy-start | bytes 76
  48.7 4.7 %copy-start.8 = (bf16[256,256]{1,0:T(8,128)(2,1)S(1)}, bf16[256,256]{1,0:T(8,128)(2,1)}, u32[]{:S(2)}) copy-start(bf16[256,256]{1,0:T(8,128)(2,1)} %param.12) | copy-start | bytes 393220
  48.7 4.7 %copy-start.9 = (f32[256]{0:T(256)S(1)}, f32[256]{0:T(256)}, u32[]{:S(2)}) copy-start(f32[256]{0:T(256)} %param.11) | copy-start | bytes 3076
  50.3 31.9 %copy-start.4 = (bf16[256,256]{1,0:T(8,128)(2,1)S(1)}, bf16[256,256]{1,0:T(8,128)(2,1)}, u32[]{:S(2)}) copy-start(bf16[256,256]{1,0:T(8,128)(2,1)} %param.15) | copy-start | bytes 393220
  50.3 31.9 %copy-start.5 = (bf16[256,256]{1,0:T(8,128)(2,1)S(1)}, bf16[256,256]{1,0:T(8,128)(2,1)}, u32[]{:S(2)}) copy-start(bf16[256,256]{1,0:T(8,128)(2,1)} %param.14) | copy-start | bytes 393220
  83.5 4.7 %collective-permute-start.6 = (bf16[1,32,16,32]{3,1,2,0:T(8,128)(2,1)S(1)}, bf16[1,32,16,32]{3,1,2,0:T(8,128)(2,1)S(1)}, u32[]{:S(2)}, u32[]{:S(2)}) collective-permute-start(bf16[1,32,16,32]{3,1,2,0:T(8,128)(2,1)S(1)} %get-tuple-element.34), channel_id=1, source_target_pairs={{0,8},{8,16},{16,24},{1,9},{9,17},{17,25},{2,10},{10,18},{18,26},{... | collective-permute-start | bytes 98312 | tf_op jit(solution)/shard_map/ppermute | solution.py:18
  85.7 7.2 %collective-permute-start.7 = (bf16[1,32,16,32]{3,1,2,0:T(8,128)(2,1)S(1)}, bf16[1,32,16,32]{3,1,2,0:T(8,128)(2,1)S(1)}, u32[]{:S(2)}, u32[]{:S(2)}) collective-permute-start(bf16[1,32,16,32]{3,1,2,0:T(8,128)(2,1)S(1)} %get-tuple-element.35), channel_id=1, source_target_pairs={{8,0},{16,8},{24,16},{9,1},{17,9},{25,17},{10,2},{18,10},{26,18},{... | collective-permute-start | bytes 98312 | tf_op jit(solution)/shard_map/ppermute | solution.py:20
  93.0 2.6 %collective-permute-start.8 = (bf16[10,1,16,32]{3,1,2,0:T(2,128)(2,1)S(1)}, bf16[10,1,16,32]{3,1,2,0:T(2,128)(2,1)S(1)}, u32[]{:S(2)}, u32[]{:S(2)}) collective-permute-start(bf16[10,1,16,32]{3,1,2,0:T(2,128)(2,1)S(1)} %get-tuple-element.28), channel_id=1, source_target_pairs={{0,4},{1,5},{2,6},{3,7},{8,12},{9,13},{10,14},{11,15},{16,20},{17,... | collective-permute-start | bytes 30728 | tf_op jit(solution)/shard_map/ppermute | solution.py:18
  94.3 3.2 %collective-permute-start.9 = (bf16[10,1,16,32]{3,1,2,0:T(2,128)(2,1)S(1)}, bf16[10,1,16,32]{3,1,2,0:T(2,128)(2,1)S(1)}, u32[]{:S(2)}, u32[]{:S(2)}) collective-permute-start(bf16[10,1,16,32]{3,1,2,0:T(2,128)(2,1)S(1)} %get-tuple-element.30), channel_id=1, source_target_pairs={{4,0},{5,1},{6,2},{7,3},{12,8},{13,9},{14,10},{15,11},{20,16},{21,... | collective-permute-start | bytes 30728 | tf_op jit(solution)/shard_map/ppermute | solution.py:20
  97.6 4.9 %collective-permute-start.10 = (bf16[10,34,1,32]{3,1,2,0:T(8,128)(2,1)S(1)}, bf16[10,34,1,32]{3,1,2,0:T(8,128)(2,1)S(1)}, u32[]{:S(2)}, u32[]{:S(2)}) collective-permute-start(bf16[10,34,1,32]{3,1,2,0:T(8,128)(2,1)S(1)} %get-tuple-element.19), channel_id=1, source_target_pairs={{0,1},{1,2},{2,3},{4,5},{5,6},{6,7},{8,9},{9,10},{10,11},{12,13},{... | collective-permute-start | bytes 65288 | tf_op jit(solution)/shard_map/ppermute | solution.py:18
  100.1 6.6 %collective-permute-start.11 = (bf16[10,34,1,32]{3,1,2,0:T(8,128)(2,1)S(1)}, bf16[10,34,1,32]{3,1,2,0:T(8,128)(2,1)S(1)}, u32[]{:S(2)}, u32[]{:S(2)}) collective-permute-start(bf16[10,34,1,32]{3,1,2,0:T(8,128)(2,1)S(1)} %get-tuple-element.20), channel_id=1, source_target_pairs={{1,0},{2,1},{3,2},{5,4},{6,5},{7,6},{9,8},{10,9},{11,10},{13,12},{... | collective-permute-start | bytes 65288 | tf_op jit(solution)/shard_map/ppermute | solution.py:20
  116.2 2.0 %copy-start.2 = (bf16[10,34,1,8,3,32]{5,3,4,1,0,2:T(8,128)(2,1)S(1)}, bf16[10,34,1,8,3,32]{5,3,4,1,0,2:T(8,128)(2,1)}, u32[]{:S(2)}) copy-start(bf16[10,34,1,8,3,32]{5,3,4,1,0,2:T(8,128)(2,1)} %copy.93) | copy-start | bytes 1566724
  116.2 2.0 %copy-start.7 = (bf16[3,3,3,32,32]{4,3,2,1,0:T(8,128)(2,1)S(1)}, bf16[3,3,3,32,32]{4,3,2,1,0:T(8,128)(2,1)}, u32[]{:S(2)}) copy-start(bf16[3,3,3,32,32]{4,3,2,1,0:T(8,128)(2,1)} %param.10) | copy-start | bytes 165892
